TPU v7x, 512 devices: a whole 4x4x16 slice. The times are simulated.
512 devices in a mesh: dp: 8 (over y, core), expert: 64 (over z, x).
Axes of the slice: x: 4, y: 4, z: 16, core: 2. Of those that a mesh axis runs over, the one named last changes fastest.
Arguments:
- tokens: bfloat16 [65536, 1920], P(('dp', 'expert')), may hold values from -10 to 10
- assignment: int32 [65536], P(('dp', 'expert')), may hold values from 0 to 63, as said below
- centroids: bfloat16 [64, 1920], P('expert'), may hold values from -0.125 to 0.125
- norm_gain: float32 [64, 1920], P('expert'), may hold values from 0.25 to 1.75
- inner_weight: bfloat16 [64, 4096, 1920], P('expert', 'dp'), may hold values from -0.125 to 0.125
- outer_weight: bfloat16 [64, 4096, 1920], P('expert', 'dp'), may hold values from -0.09375 to 0.09375
Outputs:
- layer_out: bfloat16 [65536, 1920], P(('dp', 'expert'))
Inputs may be any that keep to these rules, and one draw needn't show every extreme that they name: `assignment`: each expert is assigned exactly 128 of the tokens of the devices that share one index of dp. One device assigns at most 4 of its tokens to one expert, and every expert gets exactly 4 tokens from some device of each index of dp.
All inputs are finite; a program needn't handle non-finite values.
Results may differ from a plain program's by a relative error of at most 0.007.
Values may be sent and summed in bfloat16 or wider, within the bound.
A program may use at most 64 MiB of HBM per device.

v0:
```python
import jax
import jax.numpy as jnp
from jax import lax
from jax.sharding import PartitionSpec as P

epsilon = 1e-05


def in_one_piece(arrays, axis, split_dim, concat_dim, along):
    columns = [a.reshape(*a.shape[:along], -1) for a in arrays]
    both = jnp.concatenate(columns, axis=along)
    out, at, done = (
        lax.all_to_all(both, axis, split_axis=split_dim, concat_axis=concat_dim, tiled=True),
        0,
        [],
    )
    for a, column in zip(arrays, columns):
        slab = out[..., at : at + column.shape[along]]
        done.append(slab.reshape(*slab.shape[:along], *a.shape[along:]))
        at += column.shape[along]
    return tuple(done)


def normalize(rows_in, gain_row):
    values = rows_in.astype(jnp.float32)
    center = jnp.mean(values, axis=1, keepdims=True)
    spread = jnp.mean(jnp.square(values - center), axis=1, keepdims=True)
    return ((values - center) * lax.rsqrt(spread + epsilon) * gain_row).astype(jnp.bfloat16)


def expert_rows(normed, inner_mat, outer_mat):
    inner_act = lax.dot_general(
        normed, inner_mat, (((1,), (1,)), ((), ())), preferred_element_type=jnp.float32
    )
    hidden = jnp.maximum(inner_act, 0.0).astype(jnp.bfloat16)
    return jnp.dot(hidden, outer_mat, preferred_element_type=jnp.float32)


def body(tokens, assignment, centroids, norm_gain, inner_weight, outer_weight):
    tok_count = tokens.shape[0]
    experts = lax.axis_size("expert")
    capacity = 2 * tok_count // experts
    slot_total = experts * capacity
    expert_ids = jnp.arange(experts, dtype=jnp.int32)
    token_ids = jnp.arange(tok_count, dtype=jnp.int32)
    slot_ids = jnp.arange(slot_total, dtype=jnp.int32)
    onehot = (assignment[:, None] == expert_ids[None, :]).astype(jnp.int32)
    before = jnp.cumsum(onehot, axis=0) - onehot
    position = jnp.sum(before * onehot, axis=1)
    send_counts = jnp.sum(onehot, axis=0)
    slot_of = assignment * capacity + position
    matches = slot_of[None, :] == slot_ids[:, None]
    occupied = jnp.any(matches, axis=1)
    source_row = jnp.sum(jnp.where(matches, token_ids[None, :], 0), axis=1)
    outgoing = jnp.where(
        occupied[:, None], jnp.take(tokens, source_row, axis=0), jnp.zeros((), jnp.bfloat16)
    )
    arrived, arrived_counts = (
        lax.all_to_all(outgoing, "expert", split_axis=0, concat_axis=0, tiled=True),
        lax.all_to_all(send_counts, "expert", split_axis=0, concat_axis=0, tiled=True),
    )
    inclusive = jnp.cumsum(arrived_counts)
    offsets = inclusive - arrived_counts
    sender = jnp.sum((inclusive[None, :] <= token_ids[:, None]).astype(jnp.int32), axis=1)
    within = token_ids - offsets[sender]
    local_rows = jnp.take(arrived, sender * capacity + within, axis=0)
    inner_mat = inner_weight[0]
    outer_mat = outer_weight[0]
    partial_value = expert_rows(
        normalize(lax.all_gather(local_rows, "dp", axis=0, tiled=True), norm_gain),
        inner_mat,
        outer_mat,
    )
    expert_out = lax.psum_scatter(
        partial_value.astype(jnp.bfloat16), "dp", scatter_dimension=0, tiled=True
    )
    slot_sender = slot_ids // capacity
    slot_within = slot_ids % capacity
    slot_live = slot_within < arrived_counts[slot_sender]
    compact = jnp.where(slot_live, offsets[slot_sender] + slot_within, 0)
    returning = jnp.where(
        slot_live[:, None], jnp.take(expert_out, compact, axis=0), jnp.zeros((), jnp.bfloat16)
    )
    local_score = jnp.dot(local_rows, centroids[0], preferred_element_type=jnp.float32)
    local_gate = jax.nn.sigmoid(local_score).astype(jnp.bfloat16)
    gate_slots = jnp.where(slot_live, jnp.take(local_gate, compact), jnp.zeros((), jnp.bfloat16))
    back_rows, back_gate = in_one_piece((returning, gate_slots), "expert", 0, 0, 1)
    gate_value = jnp.take(back_gate, slot_of)
    combined = jnp.take(back_rows, slot_of, axis=0)
    mixed_out = tokens.astype(jnp.float32) + gate_value.astype(jnp.float32)[
        :, None
    ] * combined.astype(jnp.float32)
    return mixed_out.astype(jnp.bfloat16)


def solution(mesh):
    in_specs = (
        P(("dp", "expert"), None),
        P(("dp", "expert")),
        P("expert", None),
        P("expert", None),
        P("expert", "dp", None),
        P("expert", "dp", None),
    )
    out_specs = P(("dp", "expert"), None)
    return jax.shard_map(body, mesh=mesh, in_specs=in_specs, out_specs=out_specs, check_vma=False)
```

profile of v0, /device:TPU:25, one launch (start us, length us, event | category | flops | bytes accessed | tf_op | source)
XLA Modules:
  0.0 288.3 jit_solution(11351128227814640421)
XLA Ops:
  6.5 0.9 fusion.26
  7.4 0.2 reduce_window_sum.18
  7.6 0.8 fusion.27
  8.4 0.7 copy.16
  9.1 18.3 %all-to-all-start = ((s32[64,1,1]{2,1,0:T(1,128)}), s32[64,1,1]{2,1,0:T(1,128)S(1)}, u32[]{:S(2)}, u32[]{:S(2)}) async-start(s32[64,1,1]{2,1,0:T(1,128)} %copy.16), calls=%async_computation | async-start | bytes 65536 | tf_op jit(solution)/shard_map/all_to_all | solution.py:60
  27.4 0.7 compare_select_fusion.8
  28.1 0.1 select_reduce_fusion
  28.2 0.1 fusion.25
  28.4 3.4 %gather_fusion.5 = bf16[256,1920]{1,0:T(8,128)(2,1)S(1)} fusion(bf16[128,1920]{1,0:T(8,128)(2,1)} %param.10, s32[1024]{0:T(1024)S(1)} %pad_clamp_fusion.4), kind=kCustom, calls=%fused_computation.clone | custom fusion | bytes 1967104 | tf_op jit(solution)/shard_map/jit(_take)/gather | solution.py:56
  31.8 1.2 select_select_fusion.1
  33.1 2.6 all_to_all.25
  35.6 5.2 %all-to-all-done = s32[64,1,1]{2,1,0:T(1,128)S(1)} async-done(((s32[64,1,1]{2,1,0:T(1,128)}), s32[64,1,1]{2,1,0:T(1,128)S(1)}, u32[]{:S(2)}, u32[]{:S(2)}) %all-to-all-start) | async-done | bytes 288 | tf_op jit(solution)/shard_map/all_to_all | solution.py:60
  40.8 9.6 %all-to-all-start.1 = ((bf16[64,4,1920]{2,1,0:T(4,128)(2,1)}), bf16[64,4,1920]{2,1,0:T(4,128)(2,1)}, u32[]{:S(2)}, u32[]{:S(2)}) async-start(bf16[64,4,1920]{2,1,0:T(4,128)(2,1)} %all_to_all.25), calls=%async_computation.1 | async-start | bytes 1966080 | tf_op jit(solution)/shard_map/all_to_all | solution.py:59
  50.5 0.1 reduce-window.8
  50.6 0.1 reduce.1
  50.7 1.2 reduce
  52.0 1.2 gather_fusion.1
  53.3 45.7 %all-to-all-done.1 = bf16[64,4,1920]{2,1,0:T(4,128)(2,1)} async-done(((bf16[64,4,1920]{2,1,0:T(4,128)(2,1)}), bf16[64,4,1920]{2,1,0:T(4,128)(2,1)}, u32[]{:S(2)}, u32[]{:S(2)}) %all-to-all-start.1) | async-done | bytes 983072 | tf_op jit(solution)/shard_map/all_to_all | solution.py:59
  99.0 1.7 all_to_all.27
  100.7 0.9 gather_fusion.6
  101.6 0.9 broadcast_select_fusion
  102.6 0.2 reduce-scatter.2.cloned.1.call-start
  102.8 32.6 %all-gather.2.cloned.1.call-done = bf16[1024,1920]{1,0:T(8,128)(2,1)} async-done(((bf16[128,1920]{1,0:T(8,128)(2,1)}), bf16[1024,1920]{1,0:T(8,128)(2,1)}) %all-gather.2.cloned.1.call-update) | async-done | bytes 3932176 | tf_op jit(solution)/shard_map/all_gather | solution.py:70
  135.4 2.8 convert_reduce_fusion
  138.3 0.4 copy-done.2
  138.7 1.2 fusion.2
  139.9 9.2 %convolution_convert_fusion = bf16[1024,1920]{1,0:T(8,128)(2,1)} fusion(bf16[1,512,1920]{2,1,0:T(8,128)(2,1)S(1)} %copy-done, bf16[1,512,1920]{2,1,0:T(8,128)(2,1)} %param.14, bf16[1024,1920]{1,0:T(8,128)(2,1)} %all-gather.2.cloned.1.call-done, f32[1920]{0:T(1024)S(1)} %reduce.2, f32[1024]{0:T(1024)S(1)} %add_rsqrt_fusion, f32[1024]{0:T(1024)S(1)} %broadcast_multiply_fusion), kind=kOutput, calls=%fused_computation.20 | convolution fusion | flops 4039376896 | bytes 11812352 | tf_op jit(solution)/shard_map/dot_general | solution.py:36
  149.1 1.9 gather_fusion
  151.0 1.9 gather_fusion.2
  152.9 0.1 gather.37
  153.0 0.1 gather.36
  153.2 0.2 fusion.20
  153.4 1.9 gather_fusion.3
  155.3 0.1 gather.41
  155.5 0.5 copy.18
  156.0 39.2 %reduce-scatter.2.cloned.1.call-done = bf16[128,1920]{1,0:T(8,128)(2,1)} async-done(((bf16[1024,1920]{1,0:T(8,128)(2,1)}), bf16[128,1920]{1,0:T(8,128)(2,1)}) %reduce-scatter.2.cloned.1.call-update) | async-done | bytes 491536 | tf_op jit(solution)/shard_map/reduce_scatter | solution.py:74
  195.1 3.4 %gather_fusion.7 = bf16[256,1920]{1,0:T(8,128)(2,1)S(1)} fusion(bf16[128,1920]{1,0:T(8,128)(2,1)} %reduce-scatter.2.cloned.1.call-done, s32[1024]{0:T(1024)S(1)} %pad_clamp_fusion.2), kind=kCustom, calls=%fused_computation.2.clone | custom fusion | bytes 1967104 | tf_op jit(solution)/shard_map/jit(_take)/gather | solution.py:82
  198.6 1.2 select_select_fusion
  199.8 1.8 concatenate.6
  201.6 1.6 pad_maximum_fusion
  203.3 14.3 %all-to-all-start.2 = ((bf16[64,4,1921]{2,1,0:T(4,128)(2,1)}), bf16[64,4,1921]{2,1,0:T(4,128)(2,1)S(1)}, u32[]{:S(2)}, u32[]{:S(2)}) async-start(bf16[64,4,1921]{2,1,0:T(4,128)(2,1)} %pad_maximum_fusion), calls=%async_computation.3 | async-start | bytes 2097152 | tf_op jit(solution)/shard_map/all_to_all | solution.py:13
  217.6 55.2 %all-to-all-done.2 = bf16[64,4,1921]{2,1,0:T(4,128)(2,1)S(1)} async-done(((bf16[64,4,1921]{2,1,0:T(4,128)(2,1)}), bf16[64,4,1921]{2,1,0:T(4,128)(2,1)S(1)}, u32[]{:S(2)}, u32[]{:S(2)}) %all-to-all-start.2) | async-done | bytes 983584 | tf_op jit(solution)/shard_map/all_to_all | solution.py:13
  272.8 1.3 all_to_all.29
  274.1 1.3 slice.27
  275.4 0.9 slice_reduce_fusion
  276.4 1.7 gather_fusion.8
  278.1 1.2 gather_fusion.4
  279.3 2.1 add_convert_fusion
  (35 shorter events, 0.4 us)
Async XLA Ops:
  6.5 133.3 %copy-start = (bf16[1,512,1920]{2,1,0:T(8,128)(2,1)S(1)}, bf16[1,512,1920]{2,1,0:T(8,128)(2,1)}, u32[]{:S(2)}) copy-start(bf16[1,512,1920]{2,1,0:T(8,128)(2,1)} %param.15) | copy-start | bytes 5898244
  9.1 31.7 %all-to-all-start = ((s32[64,1,1]{2,1,0:T(1,128)}), s32[64,1,1]{2,1,0:T(1,128)S(1)}, u32[]{:S(2)}, u32[]{:S(2)}) async-start(s32[64,1,1]{2,1,0:T(1,128)} %copy.16), calls=%async_computation | async-start | bytes 65536 | tf_op jit(solution)/shard_map/all_to_all | solution.py:60
  40.8 58.2 %all-to-all-start.1 = ((bf16[64,4,1920]{2,1,0:T(4,128)(2,1)}), bf16[64,4,1920]{2,1,0:T(4,128)(2,1)}, u32[]{:S(2)}, u32[]{:S(2)}) async-start(bf16[64,4,1920]{2,1,0:T(4,128)(2,1)} %all_to_all.25), calls=%async_computation.1 | async-start | bytes 1966080 | tf_op jit(solution)/shard_map/all_to_all | solution.py:59
  50.4 85.0 %all-gather.2.cloned.1.call-start = ((), (), s32[]{:S(2)}) async-start(), calls=%async_computation.4 | async-start | bytes 4423680 | tf_op jit(solution)/shard_map/all_gather | solution.py:70
  53.3 49.5 %copy-start.4 = (f32[1,1920]{1,0:T(1,128)S(1)}, f32[1,1920]{1,0:T(1,128)}, u32[]{:S(2)}) copy-start(f32[1,1920]{1,0:T(1,128)} %param.13) | copy-start | bytes 23044
  102.6 92.6 %reduce-scatter.2.cloned.1.call-start = ((), (), s32[]{:S(2)}) async-start(), calls=%async_computation.5 | async-start | bytes 4423680 | tf_op jit(solution)/shard_map/reduce_scatter | solution.py:74
  135.4 3.3 %copy-start.2 = (bf16[1024,1920]{1,0:T(8,128)(2,1)S(1)}, bf16[1024,1920]{1,0:T(8,128)(2,1)}, u32[]{:S(2)}) copy-start(bf16[1024,1920]{1,0:T(8,128)(2,1)} %all-gather.2.cloned.1.call-done) | copy-start | bytes 11796484
  149.0 4.1 %copy-start.3 = (bf16[128,1920]{1,0:T(8,128)(2,1)S(1)}, bf16[128,1920]{1,0:T(8,128)(2,1)}, u32[]{:S(2)}) copy-start(bf16[128,1920]{1,0:T(8,128)(2,1)} %broadcast_select_fusion) | copy-start | bytes 1474564
  149.1 4.1 %copy-start.5 = (bf16[1,1920]{1,0:T(2,128)(2,1)S(1)}, bf16[1,1920]{1,0:T(2,128)(2,1)}, u32[]{:S(2)}) copy-start(bf16[1,1920]{1,0:T(2,128)(2,1)} %param.12) | copy-start | bytes 11524
  203.3 69.5 %all-to-all-start.2 = ((bf16[64,4,1921]{2,1,0:T(4,128)(2,1)}), bf16[64,4,1921]{2,1,0:T(4,128)(2,1)S(1)}, u32[]{:S(2)}, u32[]{:S(2)}) async-start(bf16[64,4,1921]{2,1,0:T(4,128)(2,1)} %pad_maximum_fusion), calls=%async_computation.3 | async-start | bytes 2097152 | tf_op jit(solution)/shard_map/all_to_all | solution.py:13
  274.1 5.3 %copy-start.1 = (bf16[128,1920]{1,0:T(8,128)(2,1)S(1)}, bf16[128,1920]{1,0:T(8,128)(2,1)}, u32[]{:S(2)}) copy-start(bf16[128,1920]{1,0:T(8,128)(2,1)} %param.10) | copy-start | bytes 1474564
Sparse Core Ops, SparseCore 0:
  102.7 32.6 all-gather.1
  149.2 45.8 reduce-scatter.1
where the time goes:
time: 289 us; the launch traced here: 288 us
  waiting for transfers between devices  178 us (62%)
  starting transfers between devices  42.5 us (15%)
  local copies, waits for them, and re-layouts  29.3 us (10%)
  other arithmetic  15.6 us (5%)
  between operations  13.7 us (5%)
  matrix products  9.41 us (3%)
    all_to_all x1, waiting for transfers between devices, in_one_piece(): lax.all_to_all(both, axis, split_axis=split_dim, concat_axis=concat_dim,...  55.2 us
    all_to_all x1, waiting for transfers between devices, body(): lax.all_to_all(outgoing, 'expert', split_axis=0, concat_axis=0, tiled=True)  45.7 us
    reduce_scatter x1, waiting for transfers between devices, body(): lax.psum_scatter(partial_value.astype(jnp.bfloat16), 'dp', scatter_dimens...  39.2 us
    all_gather x1, waiting for transfers between devices, body(): lax.all_gather(local_rows, 'dp', axis=0, tiled=True)  32.6 us
    all_to_all x1, starting transfers between devices, body(): lax.all_to_all(send_counts, 'expert', split_axis=0, concat_axis=0, tiled=...  18.3 us
    all_to_all x1, starting transfers between devices, in_one_piece(): lax.all_to_all(both, axis, split_axis=split_dim, concat_axis=concat_dim,...  14.3 us
    all_to_all x1, starting transfers between devices, body(): lax.all_to_all(outgoing, 'expert', split_axis=0, concat_axis=0, tiled=True)  9.56 us
    dot_general x1, matrix products, expert_rows(): return jnp.dot(hidden, outer_mat, preferred_element_type=jnp.float32)  9.17 us
  transfers between devices with their start and end apart: 5, of which 5 were waited for; matrix products, arithmetic and copies ran while one was open for 5% of the time, Pallas kernels for 0%

commit v1 on v0

--- a/solution.py
+++ b/solution.py
@@ -1,9 +1,23 @@
+import functools
 import jax
 import jax.numpy as jnp
 from jax import lax
 from jax.sharding import PartitionSpec as P
 
 epsilon = 1e-05
+
+
+def arrange_loads(payload, peer_axis):
+    lanes = lax.axis_size(peer_axis)
+    ledger = []
+    for dev in range(payload.ndim):
+        ledger.append(lanes if dev == 0 else 1)
+    return lax.all_to_all(
+        jnp.tile(payload, ledger), axis_name=peer_axis, split_axis=0, concat_axis=0, tiled=True
+    )
+
+
+map_zone = functools.partial(arrange_loads, peer_axis="dp")
 
 
 def in_one_piece(arrays, axis, split_dim, concat_dim, along):
@@ -66,11 +80,7 @@
     local_rows = jnp.take(arrived, sender * capacity + within, axis=0)
     inner_mat = inner_weight[0]
     outer_mat = outer_weight[0]
-    partial_value = expert_rows(
-        normalize(lax.all_gather(local_rows, "dp", axis=0, tiled=True), norm_gain),
-        inner_mat,
-        outer_mat,
-    )
+    partial_value = expert_rows(normalize(map_zone(local_rows), norm_gain), inner_mat, outer_mat)
     expert_out = lax.psum_scatter(
         partial_value.astype(jnp.bfloat16), "dp", scatter_dimension=0, tiled=True
     )

time: 289 us -> 307 us (1.062)
  starting transfers between devices: 42.5 us -> 51.4 us
  other arithmetic: 15.6 us -> 21 us
    all_to_all x0 -> x1, waiting for transfers between devices: none -> 44.3 us  [arrange_loads(): lax.all_to_all(jnp.tile(payload, ledger), axis_name=peer_axis, split_axis...]
    all_gather x1 -> x0, waiting for transfers between devices: 32.6 us -> none  [body(): lax.all_gather(local_rows, 'dp', axis=0, tiled=True)]
    reduce_scatter x1, waiting for transfers between devices: 39.2 us -> 29.3 us  [body(): lax.psum_scatter(partial_value.astype(jnp.bfloat16), 'dp', scatter_dimens...]
    all_to_all x0 -> x1, starting transfers between devices: none -> 9.15 us  [arrange_loads(): lax.all_to_all(jnp.tile(payload, ledger), axis_name=peer_axis, split_axis...]
    convert_element_type x0 -> x1, other arithmetic: none -> 4.17 us  [normalize(): ((values - center) * lax.rsqrt(spread + epsilon) * gain_row).astype(jnp.b...]
where the time goes in v1:
time: 307 us; the launch traced here: 306 us
  waiting for transfers between devices  180 us (59%)
  starting transfers between devices  51.4 us (17%)
  local copies, waits for them, and re-layouts  31.3 us (10%)
  other arithmetic  21 us (7%)
  between operations  13.7 us (4%)
  matrix products  9.38 us (3%)
    all_to_all x1, waiting for transfers between devices, in_one_piece(): lax.all_to_all(both, axis, split_axis=split_dim, concat_axis=concat_dim,...  55.2 us
    all_to_all x1, waiting for transfers between devices, body(): lax.all_to_all(outgoing, 'expert', split_axis=0, concat_axis=0, tiled=True)  45.8 us
    all_to_all x1, waiting for transfers between devices, arrange_loads(): lax.all_to_all(jnp.tile(payload, ledger), axis_name=peer_axis, split_axis...  44.3 us
    reduce_scatter x1, waiting for transfers between devices, body(): lax.psum_scatter(partial_value.astype(jnp.bfloat16), 'dp', scatter_dimens...  29.3 us
    all_to_all x1, starting transfers between devices, body(): lax.all_to_all(send_counts, 'expert', split_axis=0, concat_axis=0, tiled=...  18.3 us
    all_to_all x1, starting transfers between devices, in_one_piece(): lax.all_to_all(both, axis, split_axis=split_dim, concat_axis=concat_dim,...  14.4 us
    all_to_all x1, starting transfers between devices, body(): lax.all_to_all(outgoing, 'expert', split_axis=0, concat_axis=0, tiled=True)  9.56 us
    all_to_all x1, starting transfers between devices, arrange_loads(): lax.all_to_all(jnp.tile(payload, ledger), axis_name=peer_axis, split_axis...  9.15 us
  transfers between devices with their start and end apart: 5, of which 5 were waited for; matrix products, arithmetic and copies ran while one was open for 5% of the time, Pallas kernels for 0%

profile of v1, /device:TPU:25, one launch (start us, length us, event | category | flops | bytes accessed | tf_op | source)
XLA Modules:
  0.0 306.4 jit_solution(12103659754098635736)
XLA Ops:
  6.5 0.9 fusion.18
  7.4 0.2 reduce_window_sum.18
  7.6 0.8 fusion.19
  8.4 0.7 copy.16
  9.1 18.3 %all-to-all-start = ((s32[64,1,1]{2,1,0:T(1,128)}), s32[64,1,1]{2,1,0:T(1,128)S(1)}, u32[]{:S(2)}, u32[]{:S(2)}) async-start(s32[64,1,1]{2,1,0:T(1,128)} %copy.16), calls=%async_computation | async-start | bytes 65536 | tf_op jit(solution)/shard_map/all_to_all | solution.py:74
  27.4 0.7 compare_select_fusion.8
  28.1 0.1 select_reduce_fusion
  28.2 0.1 fusion.17
  28.4 3.4 %gather_fusion.5 = bf16[256,1920]{1,0:T(8,128)(2,1)S(1)} fusion(bf16[128,1920]{1,0:T(8,128)(2,1)} %param.10, s32[1024]{0:T(1024)S(1)} %pad_clamp_fusion.4), kind=kCustom, calls=%fused_computation.clone | custom fusion | bytes 1967104 | tf_op jit(solution)/shard_map/jit(_take)/gather | solution.py:70
  31.8 1.2 select_select_fusion.1
  33.1 2.6 all_to_all.29
  35.6 5.2 %all-to-all-done = s32[64,1,1]{2,1,0:T(1,128)S(1)} async-done(((s32[64,1,1]{2,1,0:T(1,128)}), s32[64,1,1]{2,1,0:T(1,128)S(1)}, u32[]{:S(2)}, u32[]{:S(2)}) %all-to-all-start) | async-done | bytes 288 | tf_op jit(solution)/shard_map/all_to_all | solution.py:74
  40.8 9.6 %all-to-all-start.1 = ((bf16[64,4,1920]{2,1,0:T(4,128)(2,1)}), bf16[64,4,1920]{2,1,0:T(4,128)(2,1)}, u32[]{:S(2)}, u32[]{:S(2)}) async-start(bf16[64,4,1920]{2,1,0:T(4,128)(2,1)} %all_to_all.29), calls=%async_computation.1 | async-start | bytes 1966080 | tf_op jit(solution)/shard_map/all_to_all | solution.py:73
  50.5 0.1 reduce.3
  50.6 1.2 reduce.2
  52.0 1.2 gather_fusion.1
  53.2 45.8 %all-to-all-done.1 = bf16[64,4,1920]{2,1,0:T(4,128)(2,1)} async-done(((bf16[64,4,1920]{2,1,0:T(4,128)(2,1)}), bf16[64,4,1920]{2,1,0:T(4,128)(2,1)}, u32[]{:S(2)}, u32[]{:S(2)}) %all-to-all-start.1) | async-done | bytes 983072 | tf_op jit(solution)/shard_map/all_to_all | solution.py:73
  99.0 1.7 all_to_all.31
  100.7 0.9 gather_fusion.6
  101.6 0.1 broadcast_select_fusion
  101.8 2.4 tile.2
  104.2 9.1 %all-to-all-start.2 = ((bf16[8,128,1920]{2,1,0:T(8,128)(2,1)}), bf16[8,128,1920]{2,1,0:T(8,128)(2,1)}, u32[]{:S(2)}, u32[]{:S(2)}) async-start(bf16[8,128,1920]{2,1,0:T(8,128)(2,1)} %tile.2), calls=%async_computation.2 | async-start | bytes 7864320 | tf_op jit(solution)/shard_map/all_to_all | solution.py:15
  113.4 44.3 %all-to-all-done.2 = bf16[8,128,1920]{2,1,0:T(8,128)(2,1)} async-done(((bf16[8,128,1920]{2,1,0:T(8,128)(2,1)}), bf16[8,128,1920]{2,1,0:T(8,128)(2,1)}, u32[]{:S(2)}, u32[]{:S(2)}) %all-to-all-start.2) | async-done | bytes 3932192 | tf_op jit(solution)/shard_map/all_to_all | solution.py:15
  157.6 2.7 convert_reduce_fusion
  160.3 3.3 %fusion.2 = f32[8,128]{1,0:T(8,128)S(1)} fusion(bf16[8,128,1920]{2,1,0:T(8,128)(2,1)} %all-to-all-done.2, f32[8,128]{1,0:T(8,128)S(1)} %broadcast_multiply_fusion), kind=kLoop, calls=%fused_computation.13 | loop fusion | flops 7863296 | bytes 3940352 | tf_op jit(solution)/shard_map/reduce_sum | solution.py:41
  163.6 4.2 %fusion.4 = bf16[8,128,1920]{2,1,0:T(8,128)(2,1)} fusion(bf16[8,128,1920]{2,1,0:T(8,128)(2,1)} %all-to-all-done.2, f32[1920]{0:T(1024)S(1)} %reduce.4, f32[8,128]{1,0:T(8,128)S(1)} %add_rsqrt_fusion, f32[8,128]{1,0:T(8,128)S(1)} %broadcast_multiply_fusion), kind=kLoop, calls=%fused_computation.15 | loop fusion | flops 9830400 | bytes 7880192 | tf_op jit(solution)/shard_map/convert_element_type | solution.py:42
  167.8 9.1 %convolution_convert_fusion = bf16[1024,1920]{1,0:T(8,128)(2,1)} fusion(bf16[1,512,1920]{2,1,0:T(8,128)(2,1)S(1)} %copy-done, bf16[1024,1920]{1,0:T(8,128)(2,1)} %bitcast.38, bf16[1,512,1920]{2,1,0:T(8,128)(2,1)} %param.14), kind=kOutput, calls=%fused_computation.16 | convolution fusion | flops 4029546496 | bytes 11796480 | tf_op jit(solution)/shard_map/dot_general | solution.py:50
  177.0 1.9 gather_fusion
  178.9 1.9 gather_fusion.2
  180.8 0.1 gather.37
  180.9 0.1 gather.36
  181.0 0.2 fusion.14
  181.3 1.9 gather_fusion.3
  183.2 0.1 gather.41
  183.4 0.5 copy.18
  183.9 29.3 %reduce-scatter.2.cloned.1.call-done = bf16[128,1920]{1,0:T(8,128)(2,1)} async-done(((bf16[1024,1920]{1,0:T(8,128)(2,1)}), bf16[128,1920]{1,0:T(8,128)(2,1)}) %reduce-scatter.2.cloned.1.call-update) | async-done | bytes 491536 | tf_op jit(solution)/shard_map/reduce_scatter | solution.py:84
  213.1 3.4 %gather_fusion.7 = bf16[256,1920]{1,0:T(8,128)(2,1)S(1)} fusion(bf16[128,1920]{1,0:T(8,128)(2,1)} %reduce-scatter.2.cloned.1.call-done, s32[1024]{0:T(1024)S(1)} %pad_clamp_fusion.2), kind=kCustom, calls=%fused_computation.2.clone | custom fusion | bytes 1967104 | tf_op jit(solution)/shard_map/jit(_take)/gather | solution.py:92
  216.6 1.2 select_select_fusion
  217.8 1.8 concatenate.6
  219.6 1.6 pad_maximum_fusion
  221.3 14.4 %all-to-all-start.3 = ((bf16[64,4,1921]{2,1,0:T(4,128)(2,1)}), bf16[64,4,1921]{2,1,0:T(4,128)(2,1)S(1)}, u32[]{:S(2)}, u32[]{:S(2)}) async-start(bf16[64,4,1921]{2,1,0:T(4,128)(2,1)} %pad_maximum_fusion), calls=%async_computation.4 | async-start | bytes 2097152 | tf_op jit(solution)/shard_map/all_to_all | solution.py:27
  235.7 55.2 %all-to-all-done.3 = bf16[64,4,1921]{2,1,0:T(4,128)(2,1)S(1)} async-done(((bf16[64,4,1921]{2,1,0:T(4,128)(2,1)}), bf16[64,4,1921]{2,1,0:T(4,128)(2,1)S(1)}, u32[]{:S(2)}, u32[]{:S(2)}) %all-to-all-start.3) | async-done | bytes 983584 | tf_op jit(solution)/shard_map/all_to_all | solution.py:27
  290.8 1.3 all_to_all.34
  292.1 1.3 slice.27
  293.5 0.9 slice_reduce_fusion
  294.4 1.7 gather_fusion.8
  296.1 1.2 gather_fusion.4
  297.4 2.1 add_convert_fusion
  (32 shorter events, 0.4 us)
Async XLA Ops:
  6.5 161.3 %copy-start = (bf16[1,512,1920]{2,1,0:T(8,128)(2,1)S(1)}, bf16[1,512,1920]{2,1,0:T(8,128)(2,1)}, u32[]{:S(2)}) copy-start(bf16[1,512,1920]{2,1,0:T(8,128)(2,1)} %param.15) | copy-start | bytes 5898244
  9.1 31.7 %all-to-all-start = ((s32[64,1,1]{2,1,0:T(1,128)}), s32[64,1,1]{2,1,0:T(1,128)S(1)}, u32[]{:S(2)}, u32[]{:S(2)}) async-start(s32[64,1,1]{2,1,0:T(1,128)} %copy.16), calls=%async_computation | async-start | bytes 65536 | tf_op jit(solution)/shard_map/all_to_all | solution.py:74
  40.8 58.2 %all-to-all-start.1 = ((bf16[64,4,1920]{2,1,0:T(4,128)(2,1)}), bf16[64,4,1920]{2,1,0:T(4,128)(2,1)}, u32[]{:S(2)}, u32[]{:S(2)}) async-start(bf16[64,4,1920]{2,1,0:T(4,128)(2,1)} %all_to_all.29), calls=%async_computation.1 | async-start | bytes 1966080 | tf_op jit(solution)/shard_map/all_to_all | solution.py:73
  104.2 9.2 %copy-start.2 = (f32[1,1920]{1,0:T(1,128)S(1)}, f32[1,1920]{1,0:T(1,128)}, u32[]{:S(2)}) copy-start(f32[1,1920]{1,0:T(1,128)} %param.13) | copy-start | bytes 23044
  104.2 53.4 %all-to-all-start.2 = ((bf16[8,128,1920]{2,1,0:T(8,128)(2,1)}), bf16[8,128,1920]{2,1,0:T(8,128)(2,1)}, u32[]{:S(2)}, u32[]{:S(2)}) async-start(bf16[8,128,1920]{2,1,0:T(8,128)(2,1)} %tile.2), calls=%async_computation.2 | async-start | bytes 7864320 | tf_op jit(solution)/shard_map/all_to_all | solution.py:15
  113.3 99.8 %reduce-scatter.2.cloned.1.call-start = ((), (), s32[]{:S(2)}) async-start(), calls=%async_computation.5 | async-start | bytes 4423680 | tf_op jit(solution)/shard_map/reduce_scatter | solution.py:84
  176.9 4.1 %copy-start.3 = (bf16[1,1920]{1,0:T(2,128)(2,1)S(1)}, bf16[1,1920]{1,0:T(2,128)(2,1)}, u32[]{:S(2)}) copy-start(bf16[1,1920]{1,0:T(2,128)(2,1)} %param.12) | copy-start | bytes 11524
  221.3 69.6 %all-to-all-start.3 = ((bf16[64,4,1921]{2,1,0:T(4,128)(2,1)}), bf16[64,4,1921]{2,1,0:T(4,128)(2,1)S(1)}, u32[]{:S(2)}, u32[]{:S(2)}) async-start(bf16[64,4,1921]{2,1,0:T(4,128)(2,1)} %pad_maximum_fusion), calls=%async_computation.4 | async-start | bytes 2097152 | tf_op jit(solution)/shard_map/all_to_all | solution.py:27
  292.1 5.3 %copy-start.1 = (bf16[128,1920]{1,0:T(8,128)(2,1)S(1)}, bf16[128,1920]{1,0:T(8,128)(2,1)}, u32[]{:S(2)}) copy-start(bf16[128,1920]{1,0:T(8,128)(2,1)} %param.10) | copy-start | bytes 1474564
Sparse Core Ops, SparseCore 0:
  177.1 36.0 reduce-scatter.1
